TPU v7x, 32 devices: a whole 2x2x4 slice. The times are simulated.
32 devices in a mesh: pts: 8 (over y, x, core), cand: 4 (over z).
Axes of the slice: x: 2, y: 2, z: 4, core: 2. Of those that a mesh axis runs over, the one named last changes fastest.
Arguments:
- points: bfloat16 [8192, 1024], P('pts'), may hold values from -6 to 6
- weights: float32 [8192], P('pts'), may hold values from 0.5 to 5
- coverage: float32 [8192], P('pts'), may hold values from -0.5 to 1
- candidates: bfloat16 [4096, 1024], P('cand'), may hold values from -6 to 6
- picks: int32 [64], replicated, may hold values from 0 to 4095
Outputs:
- gains: float32 [4096], P('cand')
- top_gains: float32 [64], replicated
- new_coverage: float32 [8192], P('pts')
All inputs are finite; a program needn't handle non-finite values.
Results may differ from a plain program's by a relative error of at most 0.0003.
Values may be sent and summed in bfloat16 or wider, within the bound.
A program may use at most 64 MiB of HBM per device.

v0:
```python
import jax
import jax.numpy as jnp
from jax import lax
from jax.sharding import PartitionSpec as P

TOPK = 64


def joined(x, axis, combine):
    everything = lax.all_gather(x, axis)
    leading = everything[0]

    def hop(k, so_far):
        return combine(so_far, everything[k])

    return lax.fori_loop(1, lax.axis_size(axis), hop, leading)


def best_values(first, second):
    return lax.top_k(jnp.concatenate([first, second]), TOPK)[0]


def on_device(points, weights, coverage, candidates, picks):
    scale = points.shape[1] ** (-0.5)
    total = points.shape[0] * lax.axis_size("pts")
    cand_rows = candidates.shape[0]
    offset = lax.axis_index("cand") * cand_rows
    sims = jnp.dot(points, candidates.T, preferred_element_type=jnp.float32) * scale
    partial_value = (
        jnp.sum(weights[:, None] * jnp.maximum(sims - coverage[:, None], 0.0), axis=0) / total
    )
    gains = lax.psum(partial_value, "pts")
    top_gains = joined(lax.top_k(gains, TOPK)[0], "cand", best_values)
    columns = offset + jnp.arange(cand_rows, dtype=jnp.int32)
    chosen = jnp.any(picks[:, None] == columns[None, :], axis=0)
    local_best = jnp.max(jnp.where(chosen[None, :], sims, -1e30), axis=1)
    best_sim = lax.pmax(local_best, "cand")
    new_coverage = jnp.maximum(coverage, best_sim)
    return (gains, top_gains, new_coverage)


def solution(mesh):
    placed = (P("pts", None), P("pts"), P("pts"), P("cand", None), P())
    return jax.shard_map(
        on_device, mesh=mesh, in_specs=placed, out_specs=(P("cand"), P(), P("pts")), check_vma=False
    )
```

profile of v0, /device:TPU:0, one launch (start us, length us, event | category | flops | bytes accessed | tf_op | source)
XLA Modules:
  0.0 56.5 jit_solution(17969848759909569890)
XLA Ops:
  0.6 0.0 copy-start
  0.7 0.9 %compare_reduce_fusion = pred[1024]{0:T(1024)(128)(4,1)S(1)} fusion(s32[1024]{0:T(1024)S(1)} %iota_add_fusion, s32[64]{0:T(128)} %param.11), kind=kLoop, calls=%fused_computation.4 | loop fusion | flops 130048 | bytes 5376 | tf_op jit(solution)/shard_map/reduce_or | solution.py:35
  1.6 0.7 %copy-done = bf16[1024,1024]{1,0:T(8,128)(2,1)S(1)} copy-done((bf16[1024,1024]{1,0:T(8,128)(2,1)S(1)}, bf16[1024,1024]{1,0:T(8,128)(2,1)}, u32[]{:S(2)}) %copy-start) | copy-done | bytes 2097176
  2.2 0.0 copy-start.3
  2.2 0.0 copy-start.2
  2.2 4.4 %select_reduce_fusion = (f32[1024]{0:T(1024)S(1)}, f32[1024]{0:T(1024)S(1)}) fusion(pred[1024]{0:T(1024)(128)(4,1)S(1)} %compare_reduce_fusion, f32[1024]{0:T(1024)} %param.9, f32[1024]{0:T(1024)} %param.8, bf16[1024,1024]{1,0:T(8,128)(2,1)S(1)} %copy-done, bf16[1024,1024]{1,0:T(8,128)(2,1)} %param.10), kind=kOutput, calls=%fused_computation.2 | convolution fusion | flops 2154821632 | bytes 4211712 | tf_op jit(solution)/shard_map/dot_general | solution.py:28
  6.6 15.2 %psum.7 = f32[1024]{0:T(1024)S(1)} all-reduce(f32[1024]{0:T(1024)S(1)} %broadcast_multiply_fusion), channel_id=1, replica_groups=mesh['pts'=8,'cand'=4] {'pts'}, use_global_device_ids=true, to_apply=%region_1.0 | all-reduce | flops 1024 | bytes 8192 | tf_op jit(solution)/shard_map/psum | solution.py:32
  21.8 0.0 copy-start.1
  21.8 4.4 %top_k.14 = (f32[1024]{0:T(1024)S(1)}, s32[1024]{0:T(1024)}) sort(f32[1024]{0:T(1024)S(1)} %psum.7, s32[1024]{0:T(1024)S(1)} %iota.11), dimensions={0}, to_apply=%region_2.0 | sort | flops 10240 | bytes 16384 | tf_op jit(solution)/shard_map/top_k | solution.py:33
  26.2 0.0 copy-done.3
  26.2 0.6 %dynamic-slice = u32[1]{0:T(128)} dynamic-slice(u32[32]{0:T(128)S(1)} %copy-done.3, u32[]{:T(128)S(6)} %add.47), dynamic_slice_sizes={1} | dynamic-slice | bytes 12
  27.5 0.1 slice_dynamic-update-slice_fusion
  27.6 11.9 %all-reduce = f32[256]{0:T(256)S(1)} all-reduce(f32[256]{0:T(256)S(1)} %slice_dynamic-update-slice_fusion), channel_id=2, replica_groups=mesh['pts'=8,'cand'=4] {'cand'}, use_global_device_ids=true, to_apply=%add | all-reduce | flops 256 | bytes 2048
  39.5 0.1 reshape.14
  39.6 8.0 %while.15 = (s32[]{:T(128)}, f32[64]{0:T(128)S(1)}, f32[4,64]{1,0:T(4,128)S(1)}, s32[]{:T(128)}, s32[]{:T(128)}, /*index=5*/s32[]{:T(128)}) while((s32[]{:T(128)}, f32[64]{0:T(128)S(1)}, f32[4,64]{1,0:T(4,128)S(1)}, s32[]{:T(128)}, s32[]{:T(128)}, /*index=5*/s32[]{:T(128)}) %tuple.41), condition=%wide.region_5.6_spmd, body=%wide.region_3.5_spmd.sunk | while | flops 1029 | bytes 4211 | solution.py:16
  39.6 0.1 pad_maximum_fusion.2
  39.7 2.6 %top_k.22 = (f32[128]{0:T(128)S(1)}, s32[128]{0:T(128)}) sort(f32[128]{0:T(128)S(1)} %pad_maximum_fusion.2, s32[128]{0:T(128)S(1)} %iota.15), dimensions={0}, to_apply=%region_4.4 | sort | flops 896 | bytes 2048 | tf_op jit(solution)/shard_map/while/body/eval_jaxpr/top_k | solution.py:20
  42.2 0.1 pad_maximum_fusion.2
  42.3 2.6 %top_k.22 = (f32[128]{0:T(128)S(1)}, s32[128]{0:T(128)}) sort(f32[128]{0:T(128)S(1)} %pad_maximum_fusion.2, s32[128]{0:T(128)S(1)} %iota.15), dimensions={0}, to_apply=%region_4.4 | sort | flops 896 | bytes 2048 | tf_op jit(solution)/shard_map/while/body/eval_jaxpr/top_k | solution.py:20
  44.9 0.1 pad_maximum_fusion.2
  45.0 2.6 %top_k.22 = (f32[128]{0:T(128)S(1)}, s32[128]{0:T(128)}) sort(f32[128]{0:T(128)S(1)} %pad_maximum_fusion.2, s32[128]{0:T(128)S(1)} %iota.15), dimensions={0}, to_apply=%region_4.4 | sort | flops 896 | bytes 2048 | tf_op jit(solution)/shard_map/while/body/eval_jaxpr/top_k | solution.py:20
  47.5 0.0 copy-start.4
  47.5 8.3 %pmax.7 = f32[1024]{0:T(1024)S(1)} all-reduce(f32[1024]{0:T(1024)S(1)} %get-tuple-element.97), channel_id=1, replica_groups=mesh['pts'=8,'cand'=4] {'cand'}, use_global_device_ids=true, to_apply=%region_8.9 | all-reduce | flops 1024 | bytes 8192 | tf_op jit(solution)/shard_map/pmax | solution.py:37
  55.9 0.0 copy-done.2
  55.9 0.6 %max.13 = f32[1024]{0:T(1024)} maximum(f32[1024]{0:T(1024)S(1)} %copy-done.2, f32[1024]{0:T(1024)S(1)} %pmax.7) | non-fusion elementwise | flops 1024 | bytes 12288 | tf_op jit(solution)/shard_map/max | solution.py:38
  56.5 0.0 copy-done.1
  56.5 0.0 copy-done.4
  (11 shorter events, 0.0 us)
Async XLA Ops:
  0.6 1.6 %copy-start = (bf16[1024,1024]{1,0:T(8,128)(2,1)S(1)}, bf16[1024,1024]{1,0:T(8,128)(2,1)}, u32[]{:S(2)}) copy-start(bf16[1024,1024]{1,0:T(8,128)(2,1)} %param.7) | copy-start | bytes 6291460
  2.2 24.0 %copy-start.3 = (u32[32]{0:T(128)S(1)}, u32[32]{0:T(128)}, u32[]{:S(2)}) copy-start(u32[32]{0:T(128)} %constant.74) | copy-start | bytes 388
  2.2 53.6 %copy-start.2 = (f32[1024]{0:T(1024)S(1)}, f32[1024]{0:T(1024)}, u32[]{:S(2)}) copy-start(f32[1024]{0:T(1024)} %param.9) | copy-start | bytes 12292
  21.8 34.7 %copy-start.1 = (f32[1024]{0:T(1024)}, f32[1024]{0:T(1024)S(1)}, u32[]{:S(2)}) copy-start(f32[1024]{0:T(1024)S(1)} %psum.7) | copy-start | bytes 12292
  47.5 8.9 %copy-start.4 = (f32[64]{0:T(128)}, f32[64]{0:T(128)S(1)}, u32[]{:S(2)}) copy-start(f32[64]{0:T(128)S(1)} %get-tuple-element.93) | copy-start | bytes 772
where the time goes:
time: 56.7 us; the launch traced here: 56.5 us
  blocking collectives  35.4 us (62%)
  other arithmetic  13.9 us (25%)
  matrix products  4.37 us (8%)
  local copies, waits for them, and re-layouts  1.48 us (3%)
  between operations  1.34 us (2%)
    psum x1, blocking collectives, on_device(): gains = lax.psum(partial_value, 'pts')  15.2 us
    unnamed x1, blocking collectives  11.9 us
    pmax x1, blocking collectives, on_device(): best_sim = lax.pmax(local_best, 'cand')  8.34 us
    top_k x3, other arithmetic, best_values(): return lax.top_k(jnp.concatenate([first, second]), TOPK)[0]  7.7 us
    top_k x1, other arithmetic, on_device(): top_gains = joined(lax.top_k(gains, TOPK)[0], 'cand', best_values)  4.43 us
    dot_general x1, matrix products, on_device(): jnp.dot(points, candidates.T, preferred_element_type=jnp.float32) * scale  4.37 us
    unnamed x13, local copies, waits for them, and re-layouts  1.37 us

commit v1 on v0

--- a/solution.py
+++ b/solution.py
@@ -29,7 +29,7 @@
     partial_value = (
         jnp.sum(weights[:, None] * jnp.maximum(sims - coverage[:, None], 0.0), axis=0) / total
     )
-    gains = lax.psum(partial_value, "pts")
+    gains = jnp.sum(lax.all_gather(partial_value, "pts"), axis=0)
     top_gains = joined(lax.top_k(gains, TOPK)[0], "cand", best_values)
     columns = offset + jnp.arange(cand_rows, dtype=jnp.int32)
     chosen = jnp.any(picks[:, None] == columns[None, :], axis=0)

time: 56.7 us -> 52.2 us (0.921)
  blocking collectives: 35.4 us -> 30.9 us
    psum x1 -> x0, blocking collectives: 15.2 us -> none  [on_device(): gains = lax.psum(partial_value, 'pts')]
    all_gather x0 -> x1, blocking collectives: none -> 10.6 us  [on_device(): gains = jnp.sum(lax.all_gather(partial_value, 'pts'), axis=0)]
where the time goes in v1:
time: 52.2 us; the launch traced here: 52 us
  blocking collectives  30.9 us (59%)
  other arithmetic  13.9 us (27%)
  matrix products  4.37 us (8%)
  local copies, waits for them, and re-layouts  1.5 us (3%)
  between operations  1.35 us (3%)
    unnamed x1, blocking collectives  11.9 us
    all_gather x1, blocking collectives, on_device(): gains = jnp.sum(lax.all_gather(partial_value, 'pts'), axis=0)  10.6 us
    pmax x1, blocking collectives, on_device(): best_sim = lax.pmax(local_best, 'cand')  8.34 us
    top_k x3, other arithmetic, best_values(): return lax.top_k(jnp.concatenate([first, second]), TOPK)[0]  7.7 us
    top_k x1, other arithmetic, on_device(): top_gains = joined(lax.top_k(gains, TOPK)[0], 'cand', best_values)  4.43 us
    dot_general x1, matrix products, on_device(): jnp.dot(points, candidates.T, preferred_element_type=jnp.float32) * scale  4.37 us
    unnamed x13, local copies, waits for them, and re-layouts  1.38 us

profile of v1, /device:TPU:0, one launch (start us, length us, event | category | flops | bytes accessed | tf_op | source)
XLA Modules:
  0.0 52.0 jit_solution(10120818668522465942)
XLA Ops:
  0.6 0.0 copy-start
  0.7 0.9 %compare_reduce_fusion = pred[1024]{0:T(1024)(128)(4,1)S(1)} fusion(s32[1024]{0:T(1024)S(1)} %iota_add_fusion, s32[64]{0:T(128)} %param.11), kind=kLoop, calls=%fused_computation.4 | loop fusion | flops 130048 | bytes 5376 | tf_op jit(solution)/shard_map/reduce_or | solution.py:35
  1.6 0.7 %copy-done = bf16[1024,1024]{1,0:T(8,128)(2,1)S(1)} copy-done((bf16[1024,1024]{1,0:T(8,128)(2,1)S(1)}, bf16[1024,1024]{1,0:T(8,128)(2,1)}, u32[]{:S(2)}) %copy-start) | copy-done | bytes 2097176
  2.2 0.0 copy-start.3
  2.2 0.0 copy-start.2
  2.2 4.4 %select_reduce_fusion = (f32[1024]{0:T(1024)S(1)}, f32[1024]{0:T(1024)S(1)}) fusion(pred[1024]{0:T(1024)(128)(4,1)S(1)} %compare_reduce_fusion, f32[1024]{0:T(1024)} %param.9, f32[1024]{0:T(1024)} %param.8, bf16[1024,1024]{1,0:T(8,128)(2,1)S(1)} %copy-done, bf16[1024,1024]{1,0:T(8,128)(2,1)} %param.10), kind=kOutput, calls=%fused_computation.2 | convolution fusion | flops 2154821632 | bytes 4211712 | tf_op jit(solution)/shard_map/dot_general | solution.py:28
  6.6 10.6 %all-gather = f32[8192]{0:T(1024)S(1)} all-gather(f32[1024]{0:T(1024)S(1)} %broadcast_multiply_fusion), channel_id=2, replica_groups=mesh['pts'=8,'cand'=4] {'pts'}, dimensions={0}, use_global_device_ids=true | all-gather | bytes 36864 | tf_op jit(solution)/shard_map/all_gather | solution.py:32
  17.3 0.0 copy-start.1
  17.3 4.4 %top_k.14 = (f32[1024]{0:T(1024)S(1)}, s32[1024]{0:T(1024)}) sort(f32[1024]{0:T(1024)S(1)} %reduce_sum.19, s32[1024]{0:T(1024)S(1)} %iota.11), dimensions={0}, to_apply=%region_2.0 | sort | flops 10240 | bytes 16384 | tf_op jit(solution)/shard_map/top_k | solution.py:33
  21.7 0.0 copy-done.3
  21.7 0.6 %dynamic-slice = u32[1]{0:T(128)} dynamic-slice(u32[32]{0:T(128)S(1)} %copy-done.3, u32[]{:T(128)S(6)} %add.45), dynamic_slice_sizes={1} | dynamic-slice | bytes 12
  23.0 0.1 slice_dynamic-update-slice_fusion
  23.1 11.9 %all-reduce = f32[256]{0:T(256)S(1)} all-reduce(f32[256]{0:T(256)S(1)} %slice_dynamic-update-slice_fusion), channel_id=3, replica_groups=mesh['pts'=8,'cand'=4] {'cand'}, use_global_device_ids=true, to_apply=%add | all-reduce | flops 256 | bytes 2048
  35.0 0.1 reshape.24
  35.1 8.0 %while.15 = (s32[]{:T(128)}, f32[64]{0:T(128)S(1)}, f32[4,64]{1,0:T(4,128)S(1)}, s32[]{:T(128)}, s32[]{:T(128)}, /*index=5*/s32[]{:T(128)}) while((s32[]{:T(128)}, f32[64]{0:T(128)S(1)}, f32[4,64]{1,0:T(4,128)S(1)}, s32[]{:T(128)}, s32[]{:T(128)}, /*index=5*/s32[]{:T(128)}) %tuple.41), condition=%wide.region_5.6_spmd, body=%wide.region_3.5_spmd.sunk | while | flops 1029 | bytes 4211 | solution.py:16
  35.1 0.1 pad_maximum_fusion.2
  35.2 2.6 %top_k.22 = (f32[128]{0:T(128)S(1)}, s32[128]{0:T(128)}) sort(f32[128]{0:T(128)S(1)} %pad_maximum_fusion.2, s32[128]{0:T(128)S(1)} %iota.15), dimensions={0}, to_apply=%region_4.4 | sort | flops 896 | bytes 2048 | tf_op jit(solution)/shard_map/while/body/eval_jaxpr/top_k | solution.py:20
  37.7 0.1 pad_maximum_fusion.2
  37.8 2.6 %top_k.22 = (f32[128]{0:T(128)S(1)}, s32[128]{0:T(128)}) sort(f32[128]{0:T(128)S(1)} %pad_maximum_fusion.2, s32[128]{0:T(128)S(1)} %iota.15), dimensions={0}, to_apply=%region_4.4 | sort | flops 896 | bytes 2048 | tf_op jit(solution)/shard_map/while/body/eval_jaxpr/top_k | solution.py:20
  40.4 0.1 pad_maximum_fusion.2
  40.5 2.6 %top_k.22 = (f32[128]{0:T(128)S(1)}, s32[128]{0:T(128)}) sort(f32[128]{0:T(128)S(1)} %pad_maximum_fusion.2, s32[128]{0:T(128)S(1)} %iota.15), dimensions={0}, to_apply=%region_4.4 | sort | flops 896 | bytes 2048 | tf_op jit(solution)/shard_map/while/body/eval_jaxpr/top_k | solution.py:20
  43.0 0.0 copy-start.4
  43.0 8.3 %pmax.7 = f32[1024]{0:T(1024)S(1)} all-reduce(f32[1024]{0:T(1024)S(1)} %get-tuple-element.97), channel_id=1, replica_groups=mesh['pts'=8,'cand'=4] {'cand'}, use_global_device_ids=true, to_apply=%region_8.9 | all-reduce | flops 1024 | bytes 8192 | tf_op jit(solution)/shard_map/pmax | solution.py:37
  51.4 0.0 copy-done.2
  51.4 0.6 %max.13 = f32[1024]{0:T(1024)} maximum(f32[1024]{0:T(1024)S(1)} %copy-done.2, f32[1024]{0:T(1024)S(1)} %pmax.7) | non-fusion elementwise | flops 1024 | bytes 12288 | tf_op jit(solution)/shard_map/max | solution.py:38
  52.0 0.0 copy-done.1
  52.0 0.0 copy-done.4
  (13 shorter events, 0.1 us)
Async XLA Ops:
  0.6 1.6 %copy-start = (bf16[1024,1024]{1,0:T(8,128)(2,1)S(1)}, bf16[1024,1024]{1,0:T(8,128)(2,1)}, u32[]{:S(2)}) copy-start(bf16[1024,1024]{1,0:T(8,128)(2,1)} %param.7) | copy-start | bytes 6291460
  2.2 19.5 %copy-start.3 = (u32[32]{0:T(128)S(1)}, u32[32]{0:T(128)}, u32[]{:S(2)}) copy-start(u32[32]{0:T(128)} %constant.74) | copy-start | bytes 388
  2.2 49.1 %copy-start.2 = (f32[1024]{0:T(1024)S(1)}, f32[1024]{0:T(1024)}, u32[]{:S(2)}) copy-start(f32[1024]{0:T(1024)} %param.9) | copy-start | bytes 12292
  17.3 34.7 %copy-start.1 = (f32[1024]{0:T(1024)}, f32[1024]{0:T(1024)S(1)}, u32[]{:S(2)}) copy-start(f32[1024]{0:T(1024)S(1)} %reduce_sum.19) | copy-start | bytes 12292
  43.0 8.9 %copy-start.4 = (f32[64]{0:T(128)}, f32[64]{0:T(128)S(1)}, u32[]{:S(2)}) copy-start(f32[64]{0:T(128)S(1)} %get-tuple-element.93) | copy-start | bytes 772
